TPU v7x, 32 devices: a whole 2x2x4 slice. The times are simulated.
32 devices in a mesh: samp: 8 (over y, x, core), snp: 4 (over z).
Axes of the slice: x: 2, y: 2, z: 4, core: 2. Of those that a mesh axis runs over, the one named last changes fastest.
Arguments:
- genotypes: bfloat16 [8192, 16384], P('samp', 'snp'), may hold values from -6 to 6
- probes: bfloat16 [8, 8192], P(None, 'samp'), may hold values from -6 to 6
- env_label: int32 [8192], P('samp'), may hold values from 0 to 7
- variances: float32 [3], replicated, may hold values from 0.25 to 1
Outputs:
- first: float32 [8, 8192], P(None, 'samp')
- second: float32 [8, 8192], P(None, 'samp')
All inputs are finite; a program needn't handle non-finite values.
Results may differ from a plain program's by a relative error of at most 0.0018.
Values may be sent and summed in bfloat16 or wider, within the bound.
No kernel may reach another device: no remote copies, remote signals or barrier semaphores. Data moves between devices by JAX's collectives and lax.ppermute only.
A program may use at most 64 MiB of HBM per device.

v0:
```python
import jax
import jax.numpy as jnp
from jax import lax
from jax.sharding import PartitionSpec as P

SNPS = 16384
PROBES = 8
ENVS = 8


def local_image(snp_panel, genotypes):
    return lax.dot_general(
        snp_panel, genotypes, (((1,), (1,)), ((), ())), preferred_element_type=jnp.float32
    )


def apply_operator(current, genotypes, onehot, variances):
    rounded = current.astype(jnp.bfloat16)
    scaled = (onehot[:, None, :] * rounded[None, :, :]).reshape(ENVS * PROBES, -1)
    panel = jnp.concatenate([rounded, scaled], axis=0)
    partial_panel = jnp.dot(panel, genotypes, preferred_element_type=jnp.float32)
    snp_panel = lax.psum(partial_panel, "samp").astype(jnp.bfloat16)
    image = local_image(snp_panel, genotypes)
    additive = image[:PROBES]
    blocks = image[PROBES:].reshape(ENVS, PROBES, -1)
    interaction = jnp.sum(onehot.astype(jnp.float32)[:, None, :] * blocks, axis=0)
    weighted = variances[0] * additive / SNPS + variances[1] * interaction / SNPS
    totals = lax.psum(weighted, "snp")
    return totals + variances[2] * current


def per_device(genotypes, probes, env_label, variances):
    labels = jnp.arange(ENVS, dtype=jnp.int32)
    onehot = (env_label[None, :] == labels[:, None]).astype(jnp.bfloat16)
    first = apply_operator(probes.astype(jnp.float32), genotypes, onehot, variances)
    second = apply_operator(first, genotypes, onehot, variances)
    return (first, second)


def solution(mesh):
    return jax.shard_map(
        per_device,
        mesh=mesh,
        in_specs=(P("samp", "snp"), P(None, "samp"), P("samp"), P()),
        out_specs=(P(None, "samp"), P(None, "samp")),
        check_vma=False,
    )
```

profile of v0, /device:TPU:0, one launch (start us, length us, event | category | flops | bytes accessed | tf_op | source)
XLA Modules:
  0.0 167.7 jit_solution(6879203342592267592)
XLA Ops:
  0.6 1.4 fusion.25
  2.1 0.7 fusion.21
  2.8 0.7 multiply_bitcast_fusion.1
  3.5 5.0 %fusion.8 = f32[72,4096]{1,0:T(8,128)S(1)} fusion(bf16[1024,4096]{1,0:T(8,128)(2,1)} %param.4, bf16[64,1024]{1,0:T(8,128)(2,1)S(1)} %multiply_bitcast_fusion.1, bf16[8,1024]{1,0:T(8,128)(2,1)} %param.5), kind=kOutput, calls=%fused_computation.10 | convolution fusion | flops 604274688 | bytes 9715712 | tf_op jit(solution)/shard_map/dot_general | solution.py:21
  8.5 0.0 copy-start
  8.5 53.0 %all-reduce.2 = bf16[72,4096]{1,0:T(8,128)(2,1)S(1)} all-reduce(f32[72,4096]{1,0:T(8,128)S(1)} %fusion.8), channel_id=1, replica_groups=mesh['samp'=8,'snp'=4] {'samp'}, use_global_device_ids=true, to_apply=%region_0.0 | all-reduce | flops 294912 | bytes 1769472 | tf_op jit(solution)/shard_map/psum | solution.py:22
  61.5 6.0 %fusion.27 = f32[72,1024]{1,0:T(8,128)S(1)} fusion(bf16[72,4096]{1,0:T(8,128)(2,1)S(1)} %all-reduce.2, bf16[1024,4096]{1,0:T(8,128)(2,1)} %param.4), kind=kOutput, calls=%fused_computation.36 | convolution fusion | flops 603979776 | bytes 9273344 | tf_op jit(solution)/shard_map/dot_general | solution.py:12
  67.6 1.2 fusion.19
  68.8 19.5 %psum.29 = f32[8,1024]{1,0:T(8,128)S(1)} all-reduce(f32[8,1024]{1,0:T(8,128)S(1)} %fusion.19), channel_id=1, replica_groups=mesh['samp'=8,'snp'=4] {'snp'}, use_global_device_ids=true, to_apply=%region_2.0 | all-reduce | flops 8192 | bytes 65536 | tf_op jit(solution)/shard_map/psum | solution.py:28
  88.3 0.0 copy-done
  88.3 0.7 fusion.24
  89.0 0.0 copy-start.1
  89.1 5.0 %fusion.12 = f32[72,4096]{1,0:T(8,128)S(1)} fusion(bf16[1024,4096]{1,0:T(8,128)(2,1)} %param.4, bf16[64,1024]{1,0:T(8,128)(2,1)S(1)} %multiply_bitcast_fusion, bf16[8,1024]{1,0:T(8,128)(2,1)S(1)} %get-tuple-element.2), kind=kOutput, calls=%fused_computation.14 | convolution fusion | flops 604274688 | bytes 9715712 | tf_op jit(solution)/shard_map/dot_general | solution.py:21
  94.1 49.2 %all-reduce.3 = bf16[72,4096]{1,0:T(8,128)(2,1)S(1)} all-reduce(f32[72,4096]{1,0:T(8,128)S(1)} %fusion.12), channel_id=1, replica_groups=mesh['samp'=8,'snp'=4] {'samp'}, use_global_device_ids=true, to_apply=%region_3.0 | all-reduce | flops 294912 | bytes 1769472 | tf_op jit(solution)/shard_map/psum | solution.py:22
  143.3 6.0 %fusion.26 = f32[72,1024]{1,0:T(8,128)S(1)} fusion(bf16[72,4096]{1,0:T(8,128)(2,1)S(1)} %all-reduce.3, bf16[1024,4096]{1,0:T(8,128)(2,1)} %param.4), kind=kOutput, calls=%fused_computation.35 | convolution fusion | flops 603979776 | bytes 9273344 | tf_op jit(solution)/shard_map/dot_general | solution.py:12
  149.4 1.2 fusion.17
  150.6 15.8 %psum.31 = f32[8,1024]{1,0:T(8,128)S(1)} all-reduce(f32[8,1024]{1,0:T(8,128)S(1)} %fusion.17), channel_id=1, replica_groups=mesh['samp'=8,'snp'=4] {'snp'}, use_global_device_ids=true, to_apply=%region_5.0 | all-reduce | flops 8192 | bytes 65536 | tf_op jit(solution)/shard_map/psum | solution.py:28
  166.4 0.0 copy-done.1
  166.4 1.3 multiply_add_fusion
  (3 shorter events, 0.1 us)
Async XLA Ops:
  8.5 79.8 %copy-start = (bf16[8,1024]{1,0:T(8,128)(2,1)S(1)}, bf16[8,1024]{1,0:T(8,128)(2,1)}, u32[]{:S(2)}) copy-start(bf16[8,1024]{1,0:T(8,128)(2,1)} %param.5) | copy-start | bytes 49156
  89.0 77.4 %copy-start.1 = (f32[8,1024]{1,0:T(8,128)}, f32[8,1024]{1,0:T(8,128)S(1)}, u32[]{:S(2)}) copy-start(f32[8,1024]{1,0:T(8,128)S(1)} %get-tuple-element.3) | copy-start | bytes 98308
where the time goes:
time: 168 us
  blocking collectives  138 us (82%)
  matrix products  22.1 us (13%)
  other arithmetic  5.97 us (4%)
    psum x2, blocking collectives, apply_operator(): snp_panel = lax.psum(partial_panel, 'samp').astype(jnp.bfloat16)  102 us
    psum x2, blocking collectives, apply_operator(): totals = lax.psum(weighted, 'snp')  35.2 us
    dot_general x2, matrix products, local_image(): lax.dot_general(snp_panel, genotypes, (((1,), (1,)), ((), ())), preferred...  12.1 us
    dot_general x2, matrix products, apply_operator(): jnp.dot(panel, genotypes, preferred_element_type=jnp.float32)  9.96 us

commit v1 on v0

--- a/solution.py
+++ b/solution.py
@@ -6,6 +6,14 @@
 SNPS = 16384
 PROBES = 8
 ENVS = 8
+
+
+def doubling_sum(value, name):
+    size, total = (lax.axis_size(name), value)
+    for far in [1 << k for k in range(size.bit_length() - 1)]:
+        swap = [(i, i ^ far) for i in range(size)]
+        total = total + lax.ppermute(total, name, swap)
+    return total
 
 
 def local_image(snp_panel, genotypes):
@@ -25,7 +33,7 @@
     blocks = image[PROBES:].reshape(ENVS, PROBES, -1)
     interaction = jnp.sum(onehot.astype(jnp.float32)[:, None, :] * blocks, axis=0)
     weighted = variances[0] * additive / SNPS + variances[1] * interaction / SNPS
-    totals = lax.psum(weighted, "snp")
+    totals = doubling_sum(weighted, "snp")
     return totals + variances[2] * current
 
 

time: 168 us -> 148 us (0.88)
  blocking collectives: 138 us -> 102 us
  waiting for transfers between devices: 0 us -> 9.13 us
  starting transfers between devices: 0 us -> 8.74 us
  matrix products: 22.1 us -> 18.9 us
    psum x2 -> x0, blocking collectives: 35.2 us -> none  [apply_operator(): totals = lax.psum(weighted, 'snp')]
    ppermute x0 -> x4, waiting for transfers between devices: none -> 9.13 us  [doubling_sum(): total = total + lax.ppermute(total, name, swap)]
    ppermute x0 -> x4, starting transfers between devices: none -> 8.74 us  [doubling_sum(): total = total + lax.ppermute(total, name, swap)]
    dot_general x2, matrix products: 9.96 us -> 6.62 us  [apply_operator(): jnp.dot(panel, genotypes, preferred_element_type=jnp.float32)]
  transfers between devices with their start and end apart: 0 -> 4, of which waited for: 0 -> 4; matrix products, arithmetic and copies ran while one was open for 0% -> 0% of each run, Pallas kernels for 0% -> 0%
where the time goes in v1:
time: 148 us; the launch traced here: 147 us
  blocking collectives  102 us (69%)
  matrix products  18.9 us (13%)
  waiting for transfers between devices  9.13 us (6%)
  starting transfers between devices  8.74 us (6%)
  other arithmetic  5.98 us (4%)
    psum x2, blocking collectives, apply_operator(): snp_panel = lax.psum(partial_panel, 'samp').astype(jnp.bfloat16)  102 us
    dot_general x2, matrix products, local_image(): lax.dot_general(snp_panel, genotypes, (((1,), (1,)), ((), ())), preferred...  12.2 us
    ppermute x4, waiting for transfers between devices, doubling_sum(): total = total + lax.ppermute(total, name, swap)  9.13 us
    ppermute x4, starting transfers between devices, doubling_sum(): total = total + lax.ppermute(total, name, swap)  8.74 us
    dot_general x2, matrix products, apply_operator(): jnp.dot(panel, genotypes, preferred_element_type=jnp.float32)  6.62 us
  transfers between devices with their start and end apart: 4, of which 4 were waited for; matrix products, arithmetic and copies ran while one was open for 0% of the time, Pallas kernels for 0%

profile of v1, /device:TPU:0, one launch (start us, length us, event | category | flops | bytes accessed | tf_op | source)
XLA Modules:
  0.0 147.3 jit_solution(5662917389011090696)
XLA Ops:
  0.6 1.4 fusion.25
  2.1 0.7 fusion.21
  2.8 0.7 multiply_bitcast_fusion.1
  3.5 5.0 %fusion.8 = f32[72,4096]{1,0:T(8,128)S(1)} fusion(bf16[1024,4096]{1,0:T(8,128)(2,1)} %param.4, bf16[64,1024]{1,0:T(8,128)(2,1)S(1)} %multiply_bitcast_fusion.1, bf16[8,1024]{1,0:T(8,128)(2,1)} %param.5), kind=kOutput, calls=%fused_computation.10 | convolution fusion | flops 604274688 | bytes 9715712 | tf_op jit(solution)/shard_map/dot_general | solution.py:29
  8.5 0.0 copy-start.1
  8.5 53.1 %all-reduce.2 = bf16[72,4096]{1,0:T(8,128)(2,1)S(1)} all-reduce(f32[72,4096]{1,0:T(8,128)S(1)} %fusion.8), channel_id=1, replica_groups=mesh['samp'=8,'snp'=4] {'samp'}, use_global_device_ids=true, to_apply=%region_0.0 | all-reduce | flops 294912 | bytes 1769472 | tf_op jit(solution)/shard_map/psum | solution.py:30
  61.6 0.0 copy-start
  61.6 6.2 %fusion.27 = f32[72,1024]{1,0:T(8,128)S(1)} fusion(bf16[72,4096]{1,0:T(8,128)(2,1)S(1)} %all-reduce.2, bf16[1024,4096]{1,0:T(8,128)(2,1)} %param.4), kind=kOutput, calls=%fused_computation.36 | convolution fusion | flops 603979776 | bytes 9273344 | tf_op jit(solution)/shard_map/dot_general | solution.py:20
  67.9 1.2 fusion.19
  69.1 1.7 %collective-permute-start = (f32[8,1024]{1,0:T(8,128)S(1)}, f32[8,1024]{1,0:T(8,128)S(1)}, u32[]{:S(2)}, u32[]{:S(2)}) collective-permute-start(f32[8,1024]{1,0:T(8,128)S(1)} %fusion.19), channel_id=1, source_target_pairs={{0,1},{1,0},{2,3},{3,2},{4,5},{5,4},{6,7},{7,6},{8,9},{9,8},{10,11... | collective-permute-start | bytes 98312 | tf_op jit(solution)/shard_map/ppermute | solution.py:15
  70.8 2.5 %collective-permute-done = f32[8,1024]{1,0:T(8,128)S(1)} collective-permute-done((f32[8,1024]{1,0:T(8,128)S(1)}, f32[8,1024]{1,0:T(8,128)S(1)}, u32[]{:S(2)}, u32[]{:S(2)}) %collective-permute-start) | collective-permute-done | bytes 32800 | tf_op jit(solution)/shard_map/ppermute | solution.py:15
  73.4 2.6 %collective-permute-start.1 = (f32[8,1024]{1,0:T(8,128)S(1)}, f32[8,1024]{1,0:T(8,128)S(1)}, u32[]{:S(2)}, u32[]{:S(2)}) collective-permute-start(f32[8,1024]{1,0:T(8,128)S(1)} %add.31), channel_id=1, source_target_pairs={{0,2},{1,3},{2,0},{3,1},{4,6},{5,7},{6,4},{7,5},{8,10},{9,11},{10,... | collective-permute-start | bytes 98312 | tf_op jit(solution)/shard_map/ppermute | solution.py:15
  75.9 2.2 %collective-permute-done.1 = f32[8,1024]{1,0:T(8,128)S(1)} collective-permute-done((f32[8,1024]{1,0:T(8,128)S(1)}, f32[8,1024]{1,0:T(8,128)S(1)}, u32[]{:S(2)}, u32[]{:S(2)}) %collective-permute-start.1) | collective-permute-done | bytes 32800 | tf_op jit(solution)/shard_map/ppermute | solution.py:15
  78.2 0.0 copy-done.1
  78.2 0.7 fusion.24
  78.9 0.0 copy-start.2
  78.9 0.0 copy-done
  78.9 1.6 %fusion.12 = f32[72,4096]{1,0:T(8,128)S(1)} fusion(bf16[1024,4096]{1,0:T(8,128)(2,1)S(1)} %copy-done, bf16[64,1024]{1,0:T(8,128)(2,1)S(1)} %multiply_bitcast_fusion, bf16[8,1024]{1,0:T(8,128)(2,1)S(1)} %get-tuple-element.2), kind=kOutput, calls=%fused_computation.14 | convolution fusion | flops 604274688 | bytes 9715712 | tf_op jit(solution)/shard_map/dot_general | solution.py:29
  80.6 49.2 %all-reduce.3 = bf16[72,4096]{1,0:T(8,128)(2,1)S(1)} all-reduce(f32[72,4096]{1,0:T(8,128)S(1)} %fusion.12), channel_id=1, replica_groups=mesh['samp'=8,'snp'=4] {'samp'}, use_global_device_ids=true, to_apply=%region_2.0 | all-reduce | flops 294912 | bytes 1769472 | tf_op jit(solution)/shard_map/psum | solution.py:30
  129.8 6.0 %fusion.26 = f32[72,1024]{1,0:T(8,128)S(1)} fusion(bf16[72,4096]{1,0:T(8,128)(2,1)S(1)} %all-reduce.3, bf16[1024,4096]{1,0:T(8,128)(2,1)} %param.4), kind=kOutput, calls=%fused_computation.35 | convolution fusion | flops 603979776 | bytes 9273344 | tf_op jit(solution)/shard_map/dot_general | solution.py:20
  135.9 1.2 fusion.17
  137.1 1.8 %collective-permute-start.2 = (f32[8,1024]{1,0:T(8,128)S(1)}, f32[8,1024]{1,0:T(8,128)S(1)}, u32[]{:S(2)}, u32[]{:S(2)}) collective-permute-start(f32[8,1024]{1,0:T(8,128)S(1)} %fusion.17), channel_id=1, source_target_pairs={{0,1},{1,0},{2,3},{3,2},{4,5},{5,4},{6,7},{7,6},{8,9},{9,8},{10,11... | collective-permute-start | bytes 98312 | tf_op jit(solution)/shard_map/ppermute | solution.py:15
  138.9 2.2 %collective-permute-done.2 = f32[8,1024]{1,0:T(8,128)S(1)} collective-permute-done((f32[8,1024]{1,0:T(8,128)S(1)}, f32[8,1024]{1,0:T(8,128)S(1)}, u32[]{:S(2)}, u32[]{:S(2)}) %collective-permute-start.2) | collective-permute-done | bytes 32800 | tf_op jit(solution)/shard_map/ppermute | solution.py:15
  141.1 2.6 %collective-permute-start.3 = (f32[8,1024]{1,0:T(8,128)S(1)}, f32[8,1024]{1,0:T(8,128)S(1)}, u32[]{:S(2)}, u32[]{:S(2)}) collective-permute-start(f32[8,1024]{1,0:T(8,128)S(1)} %add.35), channel_id=1, source_target_pairs={{0,2},{1,3},{2,0},{3,1},{4,6},{5,7},{6,4},{7,5},{8,10},{9,11},{10,... | collective-permute-start | bytes 98312 | tf_op jit(solution)/shard_map/ppermute | solution.py:15
  143.8 2.2 %collective-permute-done.3 = f32[8,1024]{1,0:T(8,128)S(1)} collective-permute-done((f32[8,1024]{1,0:T(8,128)S(1)}, f32[8,1024]{1,0:T(8,128)S(1)}, u32[]{:S(2)}, u32[]{:S(2)}) %collective-permute-start.3) | collective-permute-done | bytes 32800 | tf_op jit(solution)/shard_map/ppermute | solution.py:15
  145.9 0.0 copy-done.2
  145.9 1.3 multiply_add_fusion
  (5 shorter events, 0.1 us)
Async XLA Ops:
  8.5 69.7 %copy-start.1 = (bf16[8,1024]{1,0:T(8,128)(2,1)S(1)}, bf16[8,1024]{1,0:T(8,128)(2,1)}, u32[]{:S(2)}) copy-start(bf16[8,1024]{1,0:T(8,128)(2,1)} %param.5) | copy-start | bytes 49156
  61.6 17.3 %copy-start = (bf16[1024,4096]{1,0:T(8,128)(2,1)S(1)}, bf16[1024,4096]{1,0:T(8,128)(2,1)}, u32[]{:S(2)}) copy-start(bf16[1024,4096]{1,0:T(8,128)(2,1)} %param.4) | copy-start | bytes 25165828
  69.1 4.3 %collective-permute-start = (f32[8,1024]{1,0:T(8,128)S(1)}, f32[8,1024]{1,0:T(8,128)S(1)}, u32[]{:S(2)}, u32[]{:S(2)}) collective-permute-start(f32[8,1024]{1,0:T(8,128)S(1)} %fusion.19), channel_id=1, source_target_pairs={{0,1},{1,0},{2,3},{3,2},{4,5},{5,4},{6,7},{7,6},{8,9},{9,8},{10,11... | collective-permute-start | bytes 98312 | tf_op jit(solution)/shard_map/ppermute | solution.py:15
  73.4 4.8 %collective-permute-start.1 = (f32[8,1024]{1,0:T(8,128)S(1)}, f32[8,1024]{1,0:T(8,128)S(1)}, u32[]{:S(2)}, u32[]{:S(2)}) collective-permute-start(f32[8,1024]{1,0:T(8,128)S(1)} %add.31), channel_id=1, source_target_pairs={{0,2},{1,3},{2,0},{3,1},{4,6},{5,7},{6,4},{7,5},{8,10},{9,11},{10,... | collective-permute-start | bytes 98312 | tf_op jit(solution)/shard_map/ppermute | solution.py:15
  78.9 67.1 %copy-start.2 = (f32[8,1024]{1,0:T(8,128)}, f32[8,1024]{1,0:T(8,128)S(1)}, u32[]{:S(2)}) copy-start(f32[8,1024]{1,0:T(8,128)S(1)} %get-tuple-element.3) | copy-start | bytes 98308
  137.1 4.0 %collective-permute-start.2 = (f32[8,1024]{1,0:T(8,128)S(1)}, f32[8,1024]{1,0:T(8,128)S(1)}, u32[]{:S(2)}, u32[]{:S(2)}) collective-permute-start(f32[8,1024]{1,0:T(8,128)S(1)} %fusion.17), channel_id=1, source_target_pairs={{0,1},{1,0},{2,3},{3,2},{4,5},{5,4},{6,7},{7,6},{8,9},{9,8},{10,11... | collective-permute-start | bytes 98312 | tf_op jit(solution)/shard_map/ppermute | solution.py:15
  141.1 4.8 %collective-permute-start.3 = (f32[8,1024]{1,0:T(8,128)S(1)}, f32[8,1024]{1,0:T(8,128)S(1)}, u32[]{:S(2)}, u32[]{:S(2)}) collective-permute-start(f32[8,1024]{1,0:T(8,128)S(1)} %add.35), channel_id=1, source_target_pairs={{0,2},{1,3},{2,0},{3,1},{4,6},{5,7},{6,4},{7,5},{8,10},{9,11},{10,... | collective-permute-start | bytes 98312 | tf_op jit(solution)/shard_map/ppermute | solution.py:15
